TPU v7x, 32 devices: a whole 2x2x4 slice. The times are simulated.
32 devices in a mesh: row: 4 (over y, x), col: 4 (over z), dep: 2 (over core).
Axes of the slice: x: 2, y: 2, z: 4, core: 2. Of those that a mesh axis runs over, the one named last changes fastest.
Arguments:
- matrix: float32 [16384, 16384], P('row', ('col', 'dep')), may hold values from -6 to 6
- vectors: float32 [64, 16384], P(None, ('row', 'col')), may hold values from -0.09375 to 0.09375
Outputs:
- reduced: float32 [16384, 16384], P('row', ('col', 'dep'))
All inputs are finite; a program needn't handle non-finite values.
Results may differ from a plain program's by a relative error of at most 0.0001.
Values sent between devices are 32-bit elements; how exact they have to be, the bound alone decides.
A program may use at most 128 MiB of HBM per device.

v0:
```python
import jax
import jax.numpy as jnp
from jax import lax
from jax.sharding import PartitionSpec as P

highest = lax.Precision.HIGHEST


def broadcast(value, axis, source):
    kept = jnp.where(lax.axis_index(axis) == source, value, 0).astype(value.dtype)
    return lax.psum(kept, axis)


def contract(left, right, dims):
    return lax.dot_general(left, right, (dims, ((), ())), precision=highest)


def mask_vectors(values, first_row):
    panel_width, row_count = values.shape
    positions = first_row + lax.iota(jnp.int32, row_count)[None, :]
    reflector = lax.iota(jnp.int32, panel_width)[:, None]
    filler = jnp.where(positions == reflector + 1, 1.0, 0.0).astype(values.dtype)
    return jnp.where(positions > reflector + 1, values, filler)


def make_factor(gram):
    size_b = gram.shape[0]
    half_diag = 0.5 * jnp.diagonal(gram)
    scaled = jnp.triu(gram, 1) / half_diag[:, None]
    identity = jnp.eye(size_b, dtype=gram.dtype)
    inverse = identity - scaled
    powered = scaled
    for level in range((size_b - 1).bit_length() - 1):
        powered = jnp.dot(powered, powered, precision=highest)
        inverse = jnp.dot(inverse, identity + powered, precision=highest)
    return inverse / half_diag[None, :]


def on_device(matrix, vectors):
    rows_dev, cols_dev = matrix.shape
    row_index = lax.axis_index("row")
    gathered = lax.all_gather(vectors, "col", axis=1, tiled=True)
    row_vectors = mask_vectors(gathered, row_index * rows_dev)
    col_block = lax.axis_index("col") * lax.axis_size("dep") + lax.axis_index("dep")
    offset = col_block * cols_dev - row_index * rows_dev
    local_piece = lax.dynamic_slice_in_dim(row_vectors, offset, cols_dev, 1)
    owner_row = col_block * cols_dev // rows_dev
    col_vectors = broadcast(local_piece, "row", owner_row)
    gram_part = contract(row_vectors, row_vectors, ((1,), (1,)))
    first_part = contract(row_vectors, matrix, ((1,), (0,)))
    gram_total, first_total = lax.psum((gram_part, first_part), "row")
    factor = make_factor(gram_total)
    partial_value = contract(col_vectors, matrix, ((1,), (1,)))
    summed = lax.psum(partial_value, ("col", "dep"))
    update = contract(factor, summed, ((0,), (0,)))
    cross_term = lax.psum(contract(row_vectors, update, ((1,), (1,))), "row")
    left_terms = first_total - jnp.dot(cross_term, col_vectors, precision=highest)
    scaled_terms = contract(factor, left_terms, ((0,), (0,)))
    stacked_left = jnp.concatenate([update, row_vectors], axis=0)
    stacked_right = jnp.concatenate([col_vectors, scaled_terms], axis=0)
    return matrix - contract(stacked_left, stacked_right, ((0,), (0,)))


def solution(mesh):
    placed = (P("row", ("col", "dep")), P(None, ("row", "col")))
    return jax.shard_map(
        on_device, mesh=mesh, in_specs=placed, out_specs=P("row", ("col", "dep")), check_vma=False
    )
```

profile of v0, /device:TPU:0, one launch (start us, length us, event | category | flops | bytes accessed | tf_op | source)
XLA Modules:
  0.0 297.8 jit_solution(16607201885257769943)
XLA Ops:
  6.5 0.0 all-gather.2.cloned.1.call-start
  6.5 0.7 all-gather.2.cloned.1.call-update
  7.3 0.0 all-reduce.6.cloned.1.call-start
  7.4 32.3 %all-gather.2.cloned.1.call-done = f32[64,4096]{1,0:T(8,128)} async-done(((f32[64,1024]{1,0:T(8,128)}), f32[64,4096]{1,0:T(8,128)}) %all-gather.2.cloned.1.call-update) | async-done | bytes 1048592 | tf_op jit(solution)/shard_map/all_gather | solution.py:42
  39.6 1.4 select_select_fusion
  41.1 1.0 fusion.14
  42.0 16.2 %psum.35 = f32[64,64]{1,0:T(8,128)S(1)} all-reduce(f32[64,64]{1,0:T(8,128)S(1)} %fusion.14), channel_id=1, replica_groups=mesh['row'=4,'col'=4,'dep'=2] {'row'}, use_global_device_ids=true, to_apply=%region_0.1 | all-reduce | flops 4096 | bytes 32768 | tf_op jit(solution)/shard_map/psum | solution.py:51
  58.3 0.8 gather_fusion
  59.1 0.2 fusion.10
  59.4 0.2 fusion.15
  59.5 24.8 %fusion.20 = f32[64,2048]{1,0:T(8,128)} fusion(f32[64,4096]{1,0:T(8,128)S(1)} %select_select_fusion, f32[4096,2048]{1,0:T(8,128)} %param.2), kind=kOutput, calls=%fused_computation.39 | convolution fusion | flops 6442450944 | bytes 35127296 | tf_op jit(solution)/shard_map/dot_general | solution.py:15
  84.3 0.8 dynamic-slice_select_fusion
  85.2 0.0 all-reduce.6.cloned.1.call-update
  85.2 0.2 all-reduce.4.cloned.1.call-start
  85.4 0.2 fusion.16
  85.6 0.2 fusion.6
  85.8 0.2 fusion.7
  86.0 0.2 fusion.17
  86.2 0.2 fusion.8
  86.3 49.1 %all-reduce.6.cloned.1.call-done = (f32[64,2048]{1,0:T(8,128)}, f32[64,2048]{1,0:T(8,128)}) async-done(((f32[64,2048]{1,0:T(8,128)}, f32[64,2048]{1,0:T(8,128)}), (f32[64,2048]{1,0:T(8,128)}, f32[64,2048]{1,0:T(8,128)})) %all-reduce.6.cloned.1.call-update) | async-done | bytes 1048592 | tf_op jit(solution)/shard_map/psum | solution.py:11
  135.4 0.0 copy-start
  135.4 0.0 copy-start.1
  135.4 42.8 %fusion.18 = f32[64,4096]{1,0:T(8,128)} fusion(f32[64,2048]{1,0:T(8,128)} %get-tuple-element.5, f32[4096,2048]{1,0:T(8,128)} %param.2), kind=kOutput, calls=%fused_computation.37 | convolution fusion | flops 6442450944 | bytes 35127296 | tf_op jit(solution)/shard_map/dot_general | solution.py:15
  178.3 0.0 all-reduce.4.cloned.1.call-update
  178.3 0.2 convolution_add_fusion
  178.5 0.2 fusion.9
  178.6 0.2 convolution_divide_fusion
  178.8 59.0 %all-reduce.4.cloned.1.call-done = f32[64,4096]{1,0:T(8,128)} async-done(((f32[64,4096]{1,0:T(8,128)}), f32[64,4096]{1,0:T(8,128)}) %all-reduce.4.cloned.1.call-update) | async-done | bytes 1048592 | tf_op jit(solution)/shard_map/psum | solution.py:54
  237.8 2.2 fusion.19
  240.0 1.0 fusion.21
  241.0 16.2 %psum.39 = f32[64,64]{1,0:T(8,128)S(1)} all-reduce(f32[64,64]{1,0:T(8,128)S(1)} %fusion.21), channel_id=1, replica_groups=mesh['row'=4,'col'=4,'dep'=2] {'row'}, use_global_device_ids=true, to_apply=%region_4.5 | all-reduce | flops 4096 | bytes 32768 | tf_op jit(solution)/shard_map/psum | solution.py:56
  257.2 0.0 copy-done
  257.2 0.0 copy-done.1
  257.2 0.6 convolution_subtract_fusion.1
  257.8 0.6 fusion.22
  258.4 32.8 %convolution_subtract_fusion = f32[4096,2048]{1,0:T(8,128)} fusion(f32[4096,2048]{1,0:T(8,128)} %param.2, f32[64,4096]{1,0:T(8,128)S(1)} %select_select_fusion, f32[64,4096]{1,0:T(8,128)S(1)} %fusion.19, f32[64,2048]{1,0:T(8,128)S(1)} %fusion.22, f32[64,2048]{1,0:T(8,128)S(1)} %copy-done), kind=kOutput, calls=%fused_computation.1 | convolution fusion | flops 12894076928 | bytes 70254592 | tf_op jit(solution)/shard_map/dot_general | solution.py:15
  (4 shorter events, 0.0 us)
Async XLA Ops:
  6.5 33.1 %all-gather.2.cloned.1.call-start = ((), (), s32[]{:S(2)}) async-start(), calls=%async_computation | async-start | bytes 1310720 | tf_op jit(solution)/shard_map/all_gather | solution.py:42
  7.3 128.2 %all-reduce.6.cloned.1.call-start = ((), (), s32[]{:S(2)}) async-start(), calls=%async_computation.2 | async-start | bytes 2097152 | tf_op jit(solution)/shard_map/psum | solution.py:11
  85.2 152.6 %all-reduce.4.cloned.1.call-start = ((), (), s32[]{:S(2)}) async-start(), calls=%async_computation.1 | async-start | bytes 2097152 | tf_op jit(solution)/shard_map/psum | solution.py:54
  135.4 121.8 %copy-start = (f32[64,2048]{1,0:T(8,128)S(1)}, f32[64,2048]{1,0:T(8,128)}, u32[]{:S(2)}) copy-start(f32[64,2048]{1,0:T(8,128)} %get-tuple-element.5) | copy-start | bytes 1572868
  135.4 121.8 %copy-start.1 = (f32[64,2048]{1,0:T(8,128)S(1)}, f32[64,2048]{1,0:T(8,128)}, u32[]{:S(2)}) copy-start(f32[64,2048]{1,0:T(8,128)} %get-tuple-element.6) | copy-start | bytes 1572868
Sparse Core Ops, SparseCore 0:
  8.9 30.6 all-gather.1
  85.3 50.0 all-reduce.5
  178.4 59.3 all-reduce.3
where the time goes:
time: 298 us
  waiting for transfers between devices  141 us (47%)
  matrix products  108 us (36%)
  blocking collectives  32.4 us (11%)
  between operations  13.3 us (4%)
    dot_general x7, matrix products, contract(): return lax.dot_general(left, right, (dims, ((), ())), precision=highest)  105 us
    psum x1, waiting for transfers between devices, on_device(): summed = lax.psum(partial_value, ('col', 'dep'))  59 us
    psum x1, waiting for transfers between devices, broadcast(): return lax.psum(kept, axis)  49.1 us
    all_gather x1, waiting for transfers between devices, on_device(): gathered = lax.all_gather(vectors, 'col', axis=1, tiled=True)  32.3 us
    psum x1, blocking collectives, on_device(): gram_total, first_total = lax.psum((gram_part, first_part), 'row')  16.2 us
    psum x1, blocking collectives, on_device(): cross_term = lax.psum(contract(row_vectors, update, ((1,), (1,))), 'row')  16.2 us
  transfers between devices with their start and end apart: 3, of which 3 were waited for; matrix products, arithmetic and copies ran while one was open for 0% of the time, Pallas kernels for 0%

commit v1 on v0

--- a/solution.py
+++ b/solution.py
@@ -39,7 +39,12 @@
 def on_device(matrix, vectors):
     rows_dev, cols_dev = matrix.shape
     row_index = lax.axis_index("row")
-    gathered = lax.all_gather(vectors, "col", axis=1, tiled=True)
+    ring = [vectors]
+    for hop in range(3):
+        ring.append(lax.ppermute(ring[-1], "col", [(dev, (dev + 1) % 4) for dev in range(4)]))
+    gathered = jnp.roll(
+        jnp.concatenate(ring[::-1], axis=1), (lax.axis_index("col") + 1) * ring[0].shape[1], axis=1
+    )
     row_vectors = mask_vectors(gathered, row_index * rows_dev)
     col_block = lax.axis_index("col") * lax.axis_size("dep") + lax.axis_index("dep")
     offset = col_block * cols_dev - row_index * rows_dev

time: 298 us -> 289 us (0.970)
  waiting for transfers between devices: 141 us -> 133 us
  matrix products: 108 us -> 103 us
  starting transfers between devices: 0.26 us -> 3.28 us
    all_gather x1 -> x0, waiting for transfers between devices: 32.3 us -> none  [on_device(): gathered = lax.all_gather(vectors, 'col', axis=1, tiled=True)]
    ppermute x0 -> x3, waiting for transfers between devices: none -> 26.3 us  [on_device(): lax.ppermute(ring[-1], 'col', [(dev, (dev + 1) % 4) for dev in range(4)])]
    dot_general x7, matrix products: 105 us -> 101 us  [contract(): return lax.dot_general(left, right, (dims, ((), ())), precision=highest)]
    ppermute x0 -> x3, starting transfers between devices: none -> 3.06 us  [on_device(): lax.ppermute(ring[-1], 'col', [(dev, (dev + 1) % 4) for dev in range(4)])]
  transfers between devices with their start and end apart: 3 -> 5, of which waited for: 3 -> 5; matrix products, arithmetic and copies ran while one was open for 0% -> 0% of each run, Pallas kernels for 0% -> 0%
where the time goes in v1:
time: 289 us; the launch traced here: 288 us
  waiting for transfers between devices  133 us (46%)
  matrix products  103 us (36%)
  blocking collectives  32.2 us (11%)
  between operations  13.6 us (5%)
  starting transfers between devices  3.28 us (1%)
    dot_general x7, matrix products, contract(): return lax.dot_general(left, right, (dims, ((), ())), precision=highest)  101 us
    psum x1, waiting for transfers between devices, on_device(): summed = lax.psum(partial_value, ('col', 'dep'))  59 us
    psum x1, waiting for transfers between devices, broadcast(): return lax.psum(kept, axis)  47.8 us
    ppermute x3, waiting for transfers between devices, on_device(): lax.ppermute(ring[-1], 'col', [(dev, (dev + 1) % 4) for dev in range(4)])  26.3 us
    psum x1, blocking collectives, on_device(): cross_term = lax.psum(contract(row_vectors, update, ((1,), (1,))), 'row')  16.2 us
    psum x1, blocking collectives, on_device(): gram_total, first_total = lax.psum((gram_part, first_part), 'row')  16 us
  transfers between devices with their start and end apart: 5, of which 5 were waited for; matrix products, arithmetic and copies ran while one was open for 0% of the time, Pallas kernels for 0%

profile of v1, /device:TPU:0, one launch (start us, length us, event | category | flops | bytes accessed | tf_op | source)
XLA Modules:
  0.0 288.3 jit_solution(6949529960868423192)
XLA Ops:
  6.5 0.0 copy-start.1
  6.5 0.0 all-reduce.6.cloned.1.call-start
  6.5 3.1 %collective-permute-start = (f32[64,1024]{1,0:T(8,128)}, f32[64,1024]{1,0:T(8,128)S(1)}, u32[]{:S(2)}, u32[]{:S(2)}) collective-permute-start(f32[64,1024]{1,0:T(8,128)} %param.3), channel_id=1, source_target_pairs={{0,2},{2,4},{4,6},{6,0},{1,3},{3,5},{5,7},{7,1},{8,10},{10,12},{12... | collective-permute-start | bytes 786440 | tf_op jit(solution)/shard_map/ppermute | solution.py:44
  9.6 8.6 %collective-permute-done = f32[64,1024]{1,0:T(8,128)S(1)} collective-permute-done((f32[64,1024]{1,0:T(8,128)}, f32[64,1024]{1,0:T(8,128)S(1)}, u32[]{:S(2)}, u32[]{:S(2)}) %collective-permute-start) | collective-permute-done | bytes 262176 | tf_op jit(solution)/shard_map/ppermute | solution.py:44
  18.2 0.0 collective-permute-start.1
  18.2 9.3 %collective-permute-done.1 = f32[64,1024]{1,0:T(8,128)S(1)} collective-permute-done((f32[64,1024]{1,0:T(8,128)S(1)}, f32[64,1024]{1,0:T(8,128)S(1)}, u32[]{:S(2)}, u32[]{:S(2)}) %collective-permute-start.1) | collective-permute-done | bytes 262176 | tf_op jit(solution)/shard_map/ppermute | solution.py:44
  27.5 0.0 collective-permute-start.2
  27.5 8.4 %collective-permute-done.2 = f32[64,1024]{1,0:T(8,128)S(1)} collective-permute-done((f32[64,1024]{1,0:T(8,128)S(1)}, f32[64,1024]{1,0:T(8,128)S(1)}, u32[]{:S(2)}, u32[]{:S(2)}) %collective-permute-start.2) | collective-permute-done | bytes 262176 | tf_op jit(solution)/shard_map/ppermute | solution.py:44
  36.0 1.0 constant_dynamic-update-slice_fusion.4
  37.0 0.0 copy-done.1
  37.1 0.2 select_select_fusion
  37.3 1.0 fusion.14
  38.2 16.0 %psum.35 = f32[64,64]{1,0:T(8,128)S(1)} all-reduce(f32[64,64]{1,0:T(8,128)S(1)} %fusion.14), channel_id=1, replica_groups=mesh['row'=4,'col'=4,'dep'=2] {'row'}, use_global_device_ids=true, to_apply=%region_0.1 | all-reduce | flops 4096 | bytes 32768 | tf_op jit(solution)/shard_map/psum | solution.py:56
  54.2 0.8 gather_fusion
  55.1 0.2 fusion.10
  55.3 0.2 fusion.15
  55.5 24.8 %fusion.20 = f32[64,2048]{1,0:T(8,128)} fusion(f32[64,4096]{1,0:T(8,128)S(1)} %select_select_fusion, f32[4096,2048]{1,0:T(8,128)} %param.2), kind=kOutput, calls=%fused_computation.47 | convolution fusion | flops 6442450944 | bytes 35127296 | tf_op jit(solution)/shard_map/dot_general | solution.py:15
  80.3 0.8 dynamic-slice_select_fusion
  81.1 0.0 all-reduce.6.cloned.1.call-update
  81.2 0.2 all-reduce.4.cloned.1.call-start
  81.4 0.2 fusion.16
  81.5 0.2 fusion.6
  81.8 0.2 fusion.7
  82.0 0.2 fusion.17
  82.1 0.2 fusion.8
  82.3 47.8 %all-reduce.6.cloned.1.call-done = (f32[64,2048]{1,0:T(8,128)}, f32[64,2048]{1,0:T(8,128)}) async-done(((f32[64,2048]{1,0:T(8,128)}, f32[64,2048]{1,0:T(8,128)}), (f32[64,2048]{1,0:T(8,128)}, f32[64,2048]{1,0:T(8,128)})) %all-reduce.6.cloned.1.call-update) | async-done | bytes 1048592 | tf_op jit(solution)/shard_map/psum | solution.py:11
  130.2 38.3 %fusion.18 = f32[64,4096]{1,0:T(8,128)} fusion(f32[64,2048]{1,0:T(8,128)} %get-tuple-element.5, f32[4096,2048]{1,0:T(8,128)} %param.2), kind=kOutput, calls=%fused_computation.45 | convolution fusion | flops 6442450944 | bytes 35127296 | tf_op jit(solution)/shard_map/dot_general | solution.py:15
  168.4 0.0 all-reduce.4.cloned.1.call-update
  168.4 0.2 convolution_add_fusion
  168.6 0.2 fusion.9
  168.8 0.2 convolution_divide_fusion
  169.0 0.0 copy-start
  169.0 0.0 copy-start.2
  169.0 59.0 %all-reduce.4.cloned.1.call-done = f32[64,4096]{1,0:T(8,128)} async-done(((f32[64,4096]{1,0:T(8,128)}), f32[64,4096]{1,0:T(8,128)}) %all-reduce.4.cloned.1.call-update) | async-done | bytes 1048592 | tf_op jit(solution)/shard_map/psum | solution.py:59
  227.9 2.2 fusion.19
  230.2 1.0 fusion.21
  231.2 16.2 %psum.39 = f32[64,64]{1,0:T(8,128)S(1)} all-reduce(f32[64,64]{1,0:T(8,128)S(1)} %fusion.21), channel_id=1, replica_groups=mesh['row'=4,'col'=4,'dep'=2] {'row'}, use_global_device_ids=true, to_apply=%region_4.5 | all-reduce | flops 4096 | bytes 32768 | tf_op jit(solution)/shard_map/psum | solution.py:61
  247.4 0.0 copy-done
  247.4 0.0 copy-done.2
  247.4 0.6 convolution_subtract_fusion.1
  248.0 0.6 fusion.22
  248.6 32.8 %convolution_subtract_fusion = f32[4096,2048]{1,0:T(8,128)} fusion(f32[4096,2048]{1,0:T(8,128)} %param.2, f32[64,4096]{1,0:T(8,128)S(1)} %select_select_fusion, f32[64,4096]{1,0:T(8,128)S(1)} %fusion.19, f32[64,2048]{1,0:T(8,128)S(1)} %fusion.22, f32[64,2048]{1,0:T(8,128)S(1)} %copy-done), kind=kOutput, calls=%fused_computation.1 | convolution fusion | flops 12894076928 | bytes 70254592 | tf_op jit(solution)/shard_map/dot_general | solution.py:15
  (11 shorter events, 0.2 us)
Async XLA Ops:
  6.5 30.5 %copy-start.1 = (f32[64,1024]{1,0:T(8,128)S(1)}, f32[64,1024]{1,0:T(8,128)}, u32[]{:S(2)}) copy-start(f32[64,1024]{1,0:T(8,128)} %param.3) | copy-start | bytes 786436
  6.5 123.6 %all-reduce.6.cloned.1.call-start = ((), (), s32[]{:S(2)}) async-start(), calls=%async_computation.1 | async-start | bytes 2097152 | tf_op jit(solution)/shard_map/psum | solution.py:11
  6.5 11.7 %collective-permute-start = (f32[64,1024]{1,0:T(8,128)}, f32[64,1024]{1,0:T(8,128)S(1)}, u32[]{:S(2)}, u32[]{:S(2)}) collective-permute-start(f32[64,1024]{1,0:T(8,128)} %param.3), channel_id=1, source_target_pairs={{0,2},{2,4},{4,6},{6,0},{1,3},{3,5},{5,7},{7,1},{8,10},{10,12},{12... | collective-permute-start | bytes 786440 | tf_op jit(solution)/shard_map/ppermute | solution.py:44
  18.2 9.3 %collective-permute-start.1 = (f32[64,1024]{1,0:T(8,128)S(1)}, f32[64,1024]{1,0:T(8,128)S(1)}, u32[]{:S(2)}, u32[]{:S(2)}) collective-permute-start(f32[64,1024]{1,0:T(8,128)S(1)} %collective-permute-done), channel_id=1, source_target_pairs={{0,2},{2,4},{4,6},{6,0},{1,3},{3,5},{5,7},{7,1},{8,10},{10,12},{12... | collective-permute-start | bytes 786440 | tf_op jit(solution)/shard_map/ppermute | solution.py:44
  27.5 8.4 %collective-permute-start.2 = (f32[64,1024]{1,0:T(8,128)S(1)}, f32[64,1024]{1,0:T(8,128)S(1)}, u32[]{:S(2)}, u32[]{:S(2)}) collective-permute-start(f32[64,1024]{1,0:T(8,128)S(1)} %collective-permute-done.1), channel_id=1, source_target_pairs={{0,2},{2,4},{4,6},{6,0},{1,3},{3,5},{5,7},{7,1},{8,10},{10,12},{12... | collective-permute-start | bytes 786440 | tf_op jit(solution)/shard_map/ppermute | solution.py:44
  81.2 146.8 %all-reduce.4.cloned.1.call-start = ((), (), s32[]{:S(2)}) async-start(), calls=%async_computation | async-start | bytes 2097152 | tf_op jit(solution)/shard_map/psum | solution.py:59
  169.0 78.4 %copy-start = (f32[64,2048]{1,0:T(8,128)S(1)}, f32[64,2048]{1,0:T(8,128)}, u32[]{:S(2)}) copy-start(f32[64,2048]{1,0:T(8,128)} %get-tuple-element.5) | copy-start | bytes 1572868
  169.0 78.4 %copy-start.2 = (f32[64,2048]{1,0:T(8,128)S(1)}, f32[64,2048]{1,0:T(8,128)}, u32[]{:S(2)}) copy-start(f32[64,2048]{1,0:T(8,128)} %get-tuple-element.6) | copy-start | bytes 1572868
Sparse Core Ops, SparseCore 0:
  81.3 48.8 all-reduce.5
  168.6 59.3 all-reduce.3

commit v2 on v0

--- a/solution.py
+++ b/solution.py
@@ -8,7 +8,7 @@
 
 def broadcast(value, axis, source):
     kept = jnp.where(lax.axis_index(axis) == source, value, 0).astype(value.dtype)
-    return lax.psum(kept, axis)
+    return jnp.sum(lax.all_gather(kept, axis), axis=0)
 
 
 def contract(left, right, dims):

time: 298 us -> 279 us (0.936)
  waiting for transfers between devices: 141 us -> 125 us
  matrix products: 108 us -> 102 us
    psum x1, waiting for transfers between devices: 49.1 us -> 28 us  [on_device(): gram_total, first_total = lax.psum((gram_part, first_part), 'row')]
    dot_general x7, matrix products: 105 us -> 99 us  [contract(): return lax.dot_general(left, right, (dims, ((), ())), precision=highest)]
    all_gather x0 -> x1, waiting for transfers between devices: none -> 5.55 us  [broadcast(): return jnp.sum(lax.all_gather(kept, axis), axis=0)]
  transfers between devices with their start and end apart: 3 -> 4, of which waited for: 3 -> 4; matrix products, arithmetic and copies ran while one was open for 0% -> 11% of each run, Pallas kernels for 0% -> 0%
where the time goes in v2:
time: 279 us
  waiting for transfers between devices  125 us (45%)
  matrix products  102 us (37%)
  blocking collectives  32.6 us (12%)
  between operations  13.3 us (5%)
  other arithmetic  4.05 us (1%)
    dot_general x7, matrix products, contract(): return lax.dot_general(left, right, (dims, ((), ())), precision=highest)  99 us
    psum x1, waiting for transfers between devices, on_device(): summed = lax.psum(partial_value, ('col', 'dep'))  58.6 us
    all_gather x1, waiting for transfers between devices, on_device(): gathered = lax.all_gather(vectors, 'col', axis=1, tiled=True)  32.3 us
    psum x1, waiting for transfers between devices, on_device(): gram_total, first_total = lax.psum((gram_part, first_part), 'row')  28 us
    psum x1, blocking collectives, on_device(): cross_term = lax.psum(contract(row_vectors, update, ((1,), (1,))), 'row')  16.4 us
    psum x1, blocking collectives, on_device(): gram_total, first_total = lax.psum((gram_part, first_part), 'row')  16.2 us
  transfers between devices with their start and end apart: 4, of which 4 were waited for; matrix products, arithmetic and copies ran while one was open for 11% of the time, Pallas kernels for 0%

profile of v2, /device:TPU:0, one launch (start us, length us, event | category | flops | bytes accessed | tf_op | source)
XLA Modules:
  0.0 278.8 jit_solution(10524966903585591171)
XLA Ops:
  6.5 0.0 all-gather.4.cloned.1.call-start
  6.5 0.7 all-gather.4.cloned.1.call-update
  7.3 0.0 all-gather.6.cloned.1.call-start
  7.4 32.3 %all-gather.4.cloned.1.call-done = f32[64,4096]{1,0:T(8,128)} async-done(((f32[64,1024]{1,0:T(8,128)}), f32[64,4096]{1,0:T(8,128)}) %all-gather.4.cloned.1.call-update) | async-done | bytes 1048592 | tf_op jit(solution)/shard_map/all_gather | solution.py:42
  39.6 1.4 select_select_fusion
  41.1 1.0 fusion.14
  42.0 16.2 %psum.28 = f32[64,64]{1,0:T(8,128)S(1)} all-reduce(f32[64,64]{1,0:T(8,128)S(1)} %fusion.14), channel_id=1, replica_groups=mesh['row'=4,'col'=4,'dep'=2] {'row'}, use_global_device_ids=true, to_apply=%region_0.1 | all-reduce | flops 4096 | bytes 32768 | tf_op jit(solution)/shard_map/psum | solution.py:51
  58.3 0.8 dynamic-slice_select_fusion
  59.1 0.0 all-gather.6.cloned.1.call-update
  59.2 0.0 all-reduce.3.cloned.1.call-start
  59.2 0.8 gather_fusion
  60.0 0.2 fusion.10
  60.3 0.2 fusion.15
  60.4 0.2 fusion.16
  60.6 0.2 fusion.6
  60.8 0.2 fusion.7
  61.0 0.2 fusion.17
  61.2 0.2 fusion.8
  61.4 25.2 %fusion.20 = f32[64,2048]{1,0:T(8,128)} fusion(f32[64,4096]{1,0:T(8,128)S(1)} %select_select_fusion, f32[4096,2048]{1,0:T(8,128)} %param.2), kind=kOutput, calls=%fused_computation.39 | convolution fusion | flops 6442450944 | bytes 35127296 | tf_op jit(solution)/shard_map/dot_general | solution.py:15
  86.5 5.5 %all-gather.6.cloned.1.call-done = f32[256,2048]{1,0:T(8,128)} async-done(((f32[64,2048]{1,0:T(8,128)}), f32[256,2048]{1,0:T(8,128)}) %all-gather.6.cloned.1.call-update) | async-done | bytes 2097168 | tf_op jit(solution)/shard_map/all_gather | solution.py:11
  92.1 1.8 reduce_sum.9
  93.8 36.2 %fusion.18 = f32[64,4096]{1,0:T(8,128)} fusion(f32[64,2048]{1,0:T(8,128)S(1)} %reduce_sum.9, f32[4096,2048]{1,0:T(8,128)} %param.2), kind=kOutput, calls=%fused_computation.37 | convolution fusion | flops 6442450944 | bytes 35127296 | tf_op jit(solution)/shard_map/dot_general | solution.py:15
  130.0 0.0 all-reduce.3.cloned.1.call-update
  130.1 0.2 all-reduce.5.cloned.1.call-start
  130.3 0.2 convolution_add_fusion
  130.5 0.2 fusion.9
  130.6 0.2 convolution_divide_fusion
  130.8 0.0 all-reduce.5.cloned.1.call-update
  130.8 58.6 %all-reduce.3.cloned.1.call-done = f32[64,4096]{1,0:T(8,128)} async-done(((f32[64,4096]{1,0:T(8,128)}), f32[64,4096]{1,0:T(8,128)}) %all-reduce.3.cloned.1.call-update) | async-done | bytes 1048592 | tf_op jit(solution)/shard_map/psum | solution.py:54
  189.5 2.2 fusion.19
  191.7 1.0 fusion.21
  192.7 16.4 %psum.31 = f32[64,64]{1,0:T(8,128)S(1)} all-reduce(f32[64,64]{1,0:T(8,128)S(1)} %fusion.21), channel_id=1, replica_groups=mesh['row'=4,'col'=4,'dep'=2] {'row'}, use_global_device_ids=true, to_apply=%region_4.5 | all-reduce | flops 4096 | bytes 32768 | tf_op jit(solution)/shard_map/psum | solution.py:56
  209.1 28.0 %all-reduce.5.cloned.1.call-done = f32[64,2048]{1,0:T(8,128)} async-done(((f32[64,2048]{1,0:T(8,128)}), f32[64,2048]{1,0:T(8,128)}) %all-reduce.5.cloned.1.call-update) | async-done | bytes 524304 | tf_op jit(solution)/shard_map/psum | solution.py:51
  237.1 1.6 convolution_subtract_fusion.1
  238.8 0.6 fusion.22
  239.4 32.9 %convolution_subtract_fusion = f32[4096,2048]{1,0:T(8,128)} fusion(f32[4096,2048]{1,0:T(8,128)} %param.2, f32[64,4096]{1,0:T(8,128)S(1)} %select_select_fusion, f32[64,4096]{1,0:T(8,128)S(1)} %fusion.19, f32[64,2048]{1,0:T(8,128)S(1)} %fusion.22, f32[64,2048]{1,0:T(8,128)S(1)} %reduce_sum.9), kind=kOutput, calls=%fused_computation.1 | convolution fusion | flops 12894076928 | bytes 70254592 | tf_op jit(solution)/shard_map/dot_general | solution.py:15
  (4 shorter events, 0.0 us)
Async XLA Ops:
  6.5 33.1 %all-gather.4.cloned.1.call-start = ((), (), s32[]{:S(2)}) async-start(), calls=%async_computation | async-start | bytes 1310720 | tf_op jit(solution)/shard_map/all_gather | solution.py:42
  7.3 84.8 %all-gather.6.cloned.1.call-start = ((), (), s32[]{:S(2)}) async-start(), calls=%async_computation.3 | async-start | bytes 2621440 | tf_op jit(solution)/shard_map/all_gather | solution.py:11
  59.2 130.3 %all-reduce.3.cloned.1.call-start = ((), (), s32[]{:S(2)}) async-start(), calls=%async_computation.1 | async-start | bytes 2097152 | tf_op jit(solution)/shard_map/psum | solution.py:54
  130.1 107.1 %all-reduce.5.cloned.1.call-start = ((), (), s32[]{:S(2)}) async-start(), calls=%async_computation.2 | async-start | bytes 1048576 | tf_op jit(solution)/shard_map/psum | solution.py:51
Sparse Core Ops, SparseCore 0:
  8.9 30.6 all-gather.3
  59.3 32.7 all-gather.5
  130.2 59.2 all-reduce.2
  192.3 44.7 all-reduce.4
